TPU v7x, 32 devices: a whole 2x2x4 slice. The times are simulated.
32 devices in a mesh: grp: 2 (over x), tok: 8 (over z, y), side: 2 (over core).
Axes of the slice: x: 2, y: 2, z: 4, core: 2. Of those that a mesh axis runs over, the one named last changes fastest.
Arguments:
- hidden_in: bfloat16 [512, 3072], P(('grp', 'tok')), parts along dimension 0, may hold values from -6 to 6
- queries: bfloat16 [512, 24, 128], P(('grp', 'tok'), 'side'), parts along dimension 0, may hold values from -32 to 32
- key_new: bfloat16 [512, 4, 128], P(('grp', 'tok'), 'side'), parts along dimension 0, may hold values from -32 to 32
- value_new: bfloat16 [512, 4, 128], P(('grp', 'tok'), 'side'), parts along dimension 0, may hold values from -6 to 6
- cache_keys: bfloat16 [512, 4, 128, 128], P(('grp', 'tok'), 'side'), parts along dimension 0, may hold values from -32 to 32
- cache_values: bfloat16 [512, 4, 128, 128], P(('grp', 'tok'), 'side'), parts along dimension 0, may hold values from -6 to 6
- lengths: int32 [512], P(('grp', 'tok')), parts along dimension 0, may hold values from 1 to 128, 16384 in all
- out_weight: bfloat16 [3072, 3072], P('side', 'tok'), may hold values from -0.109375 to 0.109375
- norm_gain: float32 [3072], replicated, may hold values from 0.1 to 1.9
- router_weight: float32 [3072, 4], replicated, may hold values from -0.109375 to 0.109375
- gate_weight: bfloat16 [3072, 32768], P(None, ('tok', 'side')), may hold values from -0.109375 to 0.109375
- up_weight: bfloat16 [3072, 32768], P(None, ('tok', 'side')), may hold values from -0.109375 to 0.109375
- down_weight: bfloat16 [32768, 3072], P(('tok', 'side')), may hold values from -0.0625 to 0.0625
- routes: int32 [512, 2], P('grp'), parts along dimension 0, may hold values from 0 to 3, all different within a row; in each aligned block of 32 rows (0 to 31, 32 to 63, ...) at most 24 rows name the same one
Outputs:
- mixed: bfloat16 [512, 3072], P(('grp', 'tok')), parts along dimension 0
There are 2 independent parts, one for each index of `grp`. A program takes and returns all parts, laid end to end along the dimension named above; an argument that names none is the same for every part. Nothing has to cross between parts.
Inputs may be any that keep to these rules, and one draw needn't show every extreme that they name: Every sequence has at least one valid cache position and some sequence has 128; in each serving group the lengths sum to 16384. `routes`: each row names two different experts; among the rows of one index of tok (aligned blocks of 32 rows) no expert is named by more than 24 rows, and some expert reaches 24 in some block.
All inputs are finite; a program needn't handle non-finite values.
Results may differ from a plain program's by a relative error of at most 0.0075.
Values may be sent and summed in bfloat16 or wider, within the bound.
A program may use at most 128 MiB of HBM per device.

v0:
```python
import math

import jax
import jax.numpy as jnp
from jax import lax
from jax.sharding import PartitionSpec as P

CAP = 24


def attend(queries, key_new, value_new, cache_keys, cache_values, lengths):
    seq_count, head_count, head_width = queries.shape
    kv_count = key_new.shape[1]
    places = cache_keys.shape[2]
    scaling = 1.0 / math.sqrt(head_width)
    grouped = queries.reshape(seq_count, kv_count, head_count // kv_count, head_width)
    scores = (
        jnp.einsum("skgd,skpd->skgp", grouped, cache_keys, preferred_element_type=jnp.float32)
        * scaling
    )
    usable = jnp.arange(places, dtype=jnp.int32)[None, :] < lengths[:, None]
    scores = jnp.where(usable[:, None, None, :], scores, -jnp.inf)
    own_score = (
        jnp.einsum("skgd,skd->skg", grouped, key_new, preferred_element_type=jnp.float32) * scaling
    )
    top_score = jnp.maximum(jnp.max(scores, axis=-1), own_score)
    weights = jnp.exp(scores - top_score[..., None])
    own_weight = jnp.exp(own_score - top_score)
    totals = jnp.sum(weights, axis=-1) + own_weight
    prob_low = (weights / totals[..., None]).astype(jnp.bfloat16)
    own_low = (own_weight / totals).astype(jnp.bfloat16)
    mixture = jnp.einsum(
        "skgp,skpd->skgd", prob_low, cache_values, preferred_element_type=jnp.float32
    )
    mixture = (
        mixture
        + own_low.astype(jnp.float32)[..., None] * value_new.astype(jnp.float32)[:, :, None, :]
    )
    return mixture.astype(jnp.bfloat16).reshape(seq_count, head_count * head_width)


def gating(normed, chosen, router_weight):
    logits = jnp.dot(normed.astype(jnp.float32), router_weight, precision=lax.Precision.HIGHEST)
    expert_ids = jnp.arange(router_weight.shape[1], dtype=jnp.int32)
    picks = (chosen[:, :, None] == expert_ids[None, None, :]).astype(jnp.float32)
    chosen_logits = jnp.sum(picks * logits[:, None, :], axis=-1)
    leading = jax.nn.sigmoid(chosen_logits[:, 0] - chosen_logits[:, 1])
    gates = jnp.stack([leading, 1.0 - leading], axis=1)
    return (gates, picks)


def expert_rows(block, gate_weight, up_weight, down_weight):
    gated = jnp.dot(block, gate_weight, preferred_element_type=jnp.float32)
    upward = jnp.dot(block, up_weight, preferred_element_type=jnp.float32)
    active = (jax.nn.silu(gated) * upward).astype(jnp.bfloat16)
    return jnp.dot(active, down_weight, preferred_element_type=jnp.float32)


def local(
    hidden_in,
    queries,
    key_new,
    value_new,
    cache_keys,
    cache_values,
    lengths,
    out_weight,
    norm_gain,
    router_weight,
    gate_weight,
    up_weight,
    down_weight,
    routes,
):
    seq_rows = hidden_in.shape[0]
    model_width = hidden_in.shape[1]
    tok_count = lax.axis_size("tok")
    expert_total = router_weight.shape[1]
    replicas = tok_count // expert_total
    pieces = 1
    rows_each = seq_rows // pieces
    capacity = min(CAP, rows_each)
    first_row = lax.axis_index("tok") * seq_rows
    attn_out = attend(queries, key_new, value_new, cache_keys, cache_values, lengths)
    columns = jnp.dot(
        lax.all_gather(attn_out, "tok", axis=0, tiled=True),
        out_weight,
        preferred_element_type=jnp.float32,
    )
    partial_out = lax.all_to_all(columns, "tok", split_axis=0, concat_axis=1, tiled=True)
    projected = lax.psum(partial_out, "side")
    stream = (hidden_in.astype(jnp.float32) + projected).astype(jnp.bfloat16).astype(jnp.float32)
    normed = (
        stream * lax.rsqrt(jnp.mean(stream * stream, axis=-1, keepdims=True) + 1e-05) * norm_gain
    ).astype(jnp.bfloat16)
    chosen = lax.dynamic_slice_in_dim(routes, first_row + 0, rows_each, 0)
    gates, picks = gating(normed, chosen, router_weight)
    hits = jnp.sum(picks, axis=1)
    ranks = jnp.cumsum(hits, axis=0) - hits
    slot_ids = jnp.arange(capacity, dtype=jnp.float32)
    placed = hits[:, :, None] * (ranks[:, :, None] == slot_ids[None, None, :]).astype(jnp.float32)
    send_rows = jnp.einsum(
        "bec,bd->ecd", placed.astype(jnp.bfloat16), normed, preferred_element_type=jnp.float32
    ).astype(jnp.bfloat16)
    outgoing = jnp.repeat(send_rows, replicas, axis=0)
    arrived = lax.all_to_all(outgoing, "tok", split_axis=0, concat_axis=0, tiled=True)
    sources, slots, width_in = arrived.shape
    partial_rows = expert_rows(
        arrived.reshape(sources * slots, width_in), gate_weight, up_weight, down_weight
    )
    returned = lax.all_to_all(
        partial_rows.reshape(sources, slots, width_in),
        "tok",
        split_axis=0,
        concat_axis=0,
        tiled=True,
    )
    per_expert = jnp.sum(returned.reshape(expert_total, replicas, capacity, model_width), axis=1)
    slot_gates = (
        jnp.einsum("bk,bke->be", gates, picks, precision=lax.Precision.HIGHEST)[:, :, None] * placed
    )
    combined = jnp.einsum("bec,ecd->bd", slot_gates, per_expert, precision=lax.Precision.HIGHEST)
    combined_all = lax.psum(combined, "side")
    results = (stream + combined_all).astype(jnp.bfloat16)
    return results


def solution(mesh):
    return jax.shard_map(
        local,
        mesh=mesh,
        in_specs=(
            P(("grp", "tok"), None),
            P(("grp", "tok"), "side", None),
            P(("grp", "tok"), "side", None),
            P(("grp", "tok"), "side", None),
            P(("grp", "tok"), "side", None, None),
            P(("grp", "tok"), "side", None, None),
            P(("grp", "tok")),
            P("side", "tok"),
            P(),
            P(),
            P(None, ("tok", "side")),
            P(None, ("tok", "side")),
            P(("tok", "side"), None),
            P("grp", None),
        ),
        out_specs=P(("grp", "tok"), None),
        check_vma=False,
    )
```

profile of v0, /device:TPU:0, one launch (start us, length us, event | category | flops | bytes accessed | tf_op | source)
XLA Modules:
  0.0 225.7 jit_solution(1218781161953350367)
XLA Ops:
  6.5 0.0 copy-start
  6.5 0.0 all-reduce.3.cloned.1.call-start
  6.5 0.9 iota_compare_fusion.2
  7.4 0.7 convert_element_type.48
  8.2 1.1 fusion.10
  9.3 0.0 copy-done
  9.3 0.0 copy-start.5
  9.3 2.3 %fusion.31 = (f32[32,2,6]{2,1,0:T(2,128)S(1)}, f32[32,2,6,128]{3,2,1,0:T(8,128)S(1)}) fusion(bf16[32,2,128,128]{3,2,1,0:T(8,128)(2,1)S(1)} %copy-done, bf16[32,2,6,128]{3,0,2,1:T(8,128)(2,1)} %bitcast.37, pred[32,128]{1,0:T(8,128)(4,1)S(1)} %iota_compare_fusion.2), kind=kOutput, calls=%fused_computation.57 | convolution fusion | flops 12729984 | bytes 2397696 | tf_op jit(solution)/shard_map/skgd,skpd->skgp/dot_general | solution.py:18
  11.7 0.3 fusion.8
  11.9 0.1 fusion.30
  12.0 0.0 copy-done.5
  12.0 0.0 copy-start.1
  12.0 0.7 fusion.2
  12.7 0.1 reshape.65
  12.9 33.8 %all_gather.3 = bf16[256,1536]{1,0:T(8,128)(2,1)S(1)} all-gather(bf16[32,1536]{1,0:T(8,128)(2,1)S(1)} %reshape.65), channel_id=1, replica_groups=mesh['grp'=2,'tok'=8,'side'=2] {'tok'}, dimensions={0}, use_global_device_ids=true | all-gather | bytes 884736 | tf_op jit(solution)/shard_map/all_gather | solution.py:86
  46.7 0.0 copy-done.1
  46.7 0.6 fusion.32
  47.2 0.0 copy-start.4
  47.3 0.0 copy-start.2
  47.3 0.0 copy-start.3
  47.3 0.0 copy-start.6
  47.3 14.9 %all_to_all.29 = f32[8,32,384]{2,1,0:T(8,128)S(1)} all-to-all(f32[8,32,384]{2,1,0:T(8,128)S(1)} %bitcast.32), channel_id=1, replica_groups=mesh['grp'=2,'tok'=8,'side'=2] {'tok'}, dimensions={0} | all-to-all | bytes 786432 | tf_op jit(solution)/shard_map/all_to_all | solution.py:90
  62.2 0.8 copy.45
  63.0 0.0 all-reduce.3.cloned.1.call-update
  63.0 0.0 all-reduce.5.cloned.1.call-start
  63.1 0.0 copy-done.4
  63.1 0.1 constant_dynamic-slice_fusion
  63.2 16.9 %all-reduce.3.cloned.1.call-done = f32[32,3072]{1,0:T(8,128)} async-done(((f32[32,3072]{1,0:T(8,128)}), f32[32,3072]{1,0:T(8,128)}) %all-reduce.3.cloned.1.call-update) | async-done | bytes 393232 | tf_op jit(solution)/shard_map/psum | solution.py:91
  80.1 0.0 copy-done.2
  80.1 1.2 fusion.4
  81.3 0.0 copy-done.3
  81.3 0.0 copy-done.6
  81.3 0.3 fusion.16
  81.7 0.1 copy.35
  81.8 0.1 reduce_window_sum.11
  81.9 0.1 copy.37
  82.0 0.4 convolution_convert_fusion
  82.3 0.1 broadcast_in_dim.16
  82.5 34.9 %all_to_all.30 = bf16[8,24,3072]{2,1,0:T(8,128)(2,1)S(1)} all-to-all(bf16[8,24,3072]{2,1,0:T(8,128)(2,1)S(1)} %bitcast.29), channel_id=1, replica_groups=mesh['grp'=2,'tok'=8,'side'=2] {'tok'}, dimensions={0} | all-to-all | bytes 2359296 | tf_op jit(solution)/shard_map/all_to_all | solution.py:106
  117.4 8.4 %fusion.33 = f32[192,2048]{1,0:T(8,128)} fusion(bf16[192,3072]{1,0:T(8,128)(2,1)S(1)} %bitcast.34, bf16[3072,2048]{1,0:T(8,128)(2,1)} %param.24), kind=kOutput, calls=%fused_computation.59 | convolution fusion | flops 2415919104 | bytes 15335424 | tf_op jit(solution)/shard_map/dot_general | solution.py:53
  125.8 15.3 %fusion.3 = f32[192,3072]{1,0:T(8,128)} fusion(bf16[2048,3072]{1,0:T(8,128)(2,1)} %param.26, bf16[192,3072]{1,0:T(8,128)(2,1)S(1)} %bitcast.35, bf16[3072,2048]{1,0:T(8,128)(2,1)} %param.25, f32[192,2048]{1,0:T(8,128)} %fusion.33), kind=kOutput, calls=%fused_computation.9 | convolution fusion | flops 4834197504 | bytes 30277632 | tf_op jit(solution)/shard_map/dot_general | solution.py:56
  141.1 57.0 %all_to_all.31 = f32[8,24,3072]{2,1,0:T(8,128)S(1)} all-to-all(f32[8,24,3072]{2,1,0:T(8,128)} %bitcast.30), channel_id=1, replica_groups=mesh['grp'=2,'tok'=8,'side'=2] {'tok'}, dimensions={0} | all-to-all | bytes 4718592 | tf_op jit(solution)/shard_map/all_to_all | solution.py:111
  198.1 0.1 bitcast_reduce_fusion
  198.3 1.5 convolution_bitcast_fusion
  199.7 0.0 all-reduce.5.cloned.1.call-update
  199.7 17.5 %all-reduce.5.cloned.1.call-done = f32[32,3072]{1,0:T(8,128)} async-done(((f32[32,3072]{1,0:T(8,128)}), f32[32,3072]{1,0:T(8,128)}) %all-reduce.5.cloned.1.call-update) | async-done | bytes 393232 | tf_op jit(solution)/shard_map/psum | solution.py:123
  217.2 1.7 fusion.7
  (7 shorter events, 0.1 us)
Async XLA Ops:
  6.5 2.7 %copy-start = (bf16[32,2,128,128]{3,2,1,0:T(8,128)(2,1)S(1)}, bf16[32,2,128,128]{3,2,1,0:T(8,128)(2,1)}, u32[]{:S(2)}) copy-start(bf16[32,2,128,128]{3,2,1,0:T(8,128)(2,1)} %param.18) | copy-start | bytes 6291460
  6.5 73.6 %all-reduce.3.cloned.1.call-start = ((), (), s32[]{:S(2)}) async-start(), calls=%async_computation.3 | async-start | bytes 786432 | tf_op jit(solution)/shard_map/psum | solution.py:91
  9.3 2.7 %copy-start.5 = (bf16[32,2,128,128]{3,2,1,0:T(8,128)(2,1)S(1)}, bf16[32,2,128,128]{3,2,1,0:T(8,128)(2,1)}, u32[]{:S(2)}) copy-start(bf16[32,2,128,128]{3,2,1,0:T(8,128)(2,1)} %param.19) | copy-start | bytes 6291460
  12.0 34.7 %copy-start.1 = (bf16[1536,384]{1,0:T(8,128)(2,1)S(1)}, bf16[1536,384]{1,0:T(8,128)(2,1)}, u32[]{:S(2)}) copy-start(bf16[1536,384]{1,0:T(8,128)(2,1)} %param.21) | copy-start | bytes 3538948
  47.2 15.8 %copy-start.4 = (s32[256,2]{0,1:T(2,128)S(1)}, s32[256,2]{0,1:T(2,128)}, u32[]{:S(2)}) copy-start(s32[256,2]{0,1:T(2,128)} %param.27) | copy-start | bytes 6148
  47.3 32.9 %copy-start.2 = (bf16[32,3072]{1,0:T(8,128)(2,1)S(1)}, bf16[32,3072]{1,0:T(8,128)(2,1)}, u32[]{:S(2)}) copy-start(bf16[32,3072]{1,0:T(8,128)(2,1)} %param.14) | copy-start | bytes 589828
  47.3 34.0 %copy-start.3 = (f32[3072]{0:T(1024)S(1)}, f32[3072]{0:T(1024)}, u32[]{:S(2)}) copy-start(f32[3072]{0:T(1024)} %param.22) | copy-start | bytes 36868
  47.3 34.0 %copy-start.6 = (f32[3072,4]{0,1:T(4,128)S(1)}, f32[3072,4]{0,1:T(4,128)}, u32[]{:S(2)}) copy-start(f32[3072,4]{0,1:T(4,128)} %param.23) | copy-start | bytes 147460
  63.0 154.2 %all-reduce.5.cloned.1.call-start = ((), (), s32[]{:S(2)}) async-start(), calls=%async_computation.4 | async-start | bytes 786432 | tf_op jit(solution)/shard_map/psum | solution.py:123
Sparse Core Ops, SparseCore 0:
  63.1 16.9 all-reduce.2
  199.9 17.2 all-reduce.4
where the time goes:
time: 226 us
  blocking collectives  141 us (62%)
  waiting for transfers between devices  34.4 us (15%)
  matrix products  30.5 us (13%)
  between operations  13.6 us (6%)
  other arithmetic  5.14 us (2%)
    all_to_all x1, blocking collectives, local(): lax.all_to_all(partial_rows.reshape(sources, slots, width_in), 'tok', spl...  57 us
    all_to_all x1, blocking collectives, local(): lax.all_to_all(outgoing, 'tok', split_axis=0, concat_axis=0, tiled=True)  34.9 us
    all_gather x1, blocking collectives, local(): lax.all_gather(attn_out, 'tok', axis=0, tiled=True)  33.8 us
    psum x1, waiting for transfers between devices, local(): combined_all = lax.psum(combined, 'side')  17.5 us
    psum x1, waiting for transfers between devices, local(): projected = lax.psum(partial_out, 'side')  16.9 us
    dot_general x1, matrix products, expert_rows(): return jnp.dot(active, down_weight, preferred_element_type=jnp.float32)  15.3 us
    all_to_all x1, blocking collectives, local(): lax.all_to_all(columns, 'tok', split_axis=0, concat_axis=1, tiled=True)  14.9 us
    dot_general x1, matrix products, expert_rows(): gated = jnp.dot(block, gate_weight, preferred_element_type=jnp.float32)  8.39 us
  transfers between devices with their start and end apart: 2, of which 2 were waited for; matrix products, arithmetic and copies ran while one was open for 0% of the time, Pallas kernels for 0%

commit v1 on v0

v1 whole, which is shorter than its diff:
```python
import functools
import math

import jax
import jax.numpy as jnp
from jax import lax
from jax.experimental import pallas as pl
from jax.experimental.pallas import tpu as pltpu
from jax.sharding import PartitionSpec as P

CAP = 24


def attend(queries, key_new, value_new, cache_keys, cache_values, lengths):
    seq_count, head_count, head_width = queries.shape
    kv_count = key_new.shape[1]
    places = cache_keys.shape[2]
    scaling = 1.0 / math.sqrt(head_width)
    grouped = queries.reshape(seq_count, kv_count, head_count // kv_count, head_width)
    scores = (
        jnp.einsum("skgd,skpd->skgp", grouped, cache_keys, preferred_element_type=jnp.float32)
        * scaling
    )
    usable = jnp.arange(places, dtype=jnp.int32)[None, :] < lengths[:, None]
    scores = jnp.where(usable[:, None, None, :], scores, -jnp.inf)
    own_score = (
        jnp.einsum("skgd,skd->skg", grouped, key_new, preferred_element_type=jnp.float32) * scaling
    )
    top_score = jnp.maximum(jnp.max(scores, axis=-1), own_score)
    weights = jnp.exp(scores - top_score[..., None])
    own_weight = jnp.exp(own_score - top_score)
    totals = jnp.sum(weights, axis=-1) + own_weight
    prob_low = (weights / totals[..., None]).astype(jnp.bfloat16)
    own_low = (own_weight / totals).astype(jnp.bfloat16)
    mixture = jnp.einsum(
        "skgp,skpd->skgd", prob_low, cache_values, preferred_element_type=jnp.float32
    )
    mixture = (
        mixture
        + own_low.astype(jnp.float32)[..., None] * value_new.astype(jnp.float32)[:, :, None, :]
    )
    return mixture.astype(jnp.bfloat16).reshape(seq_count, head_count * head_width)

def wire(block):
    rows, width = block.shape
    extra = rows - 16
    half = width // 2
    tail = jnp.concatenate([block[16:, :half], block[16:, half:]], axis=0)
    return jnp.concatenate([block[:16], tail], axis=1).astype(jnp.bfloat16)


def unwire(block, width):
    half = width // 2
    full = block.astype(jnp.float32)
    tail = jnp.concatenate([full[:8, width:], full[8:, width:]], axis=1)
    return jnp.concatenate([full[:, :width], tail], axis=0)


def body(
    dims,
    attn_ref,
    hidden_ref,
    routes_ref,
    routes_t_ref,
    gain_ref,
    router_ref,
    out_w_ref,
    gate_hbm,
    up_hbm,
    down_hbm,
    out_ref,
    heads,
    proj,
    proj_peer,
    cols,
    cols_in,
    stream_buf,
    tokens,
    packed,
    active,
    gate_w,
    up_w,
    down_w,
    mine,
    theirs,
    theirs_in,
    y_out,
    y_in,
    z_out,
    z_in,
    final,
    w_sem,
    ag_zs,
    ag_zr,
    ag_ys,
    ag_yr,
    tok_s,
    tok_r,
    col_s,
    col_r,
    one_s,
    one_r,
    rz_s,
    rz_r,
    ry_s,
    ry_r,
):
    T, Z, R, rows, cap = dims
    half_rows = rows // 2
    D = hidden_ref.shape[1]
    half_d = D // 2
    total = T * rows
    slots = T * cap
    part = Z * cap
    hid = gate_w.shape[1]
    tok = lax.axis_index("tok")
    side = lax.axis_index("side")
    z = tok // R
    r = tok % R
    other = 1 - side

    def zo(d):
        return (z + d) % Z

    def ro(d):
        return (r + d) % R

    def copy(src, dst, ssem, rsem, t=None, s=None):
        where = {"tok": tok if t is None else t, "side": side if s is None else s}
        return pltpu.make_async_remote_copy(
            src_ref=src,
            dst_ref=dst,
            send_sem=ssem,
            recv_sem=rsem,
            device_id=where,
            device_id_type=pl.DeviceIdType.MESH,
        )

    loads = [
        pltpu.make_async_copy(gate_hbm, gate_w, w_sem.at[0]),
        pltpu.make_async_copy(up_hbm, up_w, w_sem.at[1]),
        pltpu.make_async_copy(down_hbm, down_w, w_sem.at[2]),
    ]
    for load in loads:
        load.start()

    barrier = pltpu.get_barrier_semaphore()
    for d in range(1, T):
        pl.semaphore_signal(
            barrier,
            inc=1,
            device_id={"tok": (tok + d) % T, "side": side},
            device_id_type=pl.DeviceIdType.MESH,
        )
    pl.semaphore_signal(
        barrier, inc=1, device_id={"tok": tok, "side": other}, device_id_type=pl.DeviceIdType.MESH
    )
    pl.semaphore_wait(barrier, T)

    z_order = sorted(range(1, Z), key=lambda d: -min(d, Z - d))
    z_wait = z_order[::-1]
    pending = []

    def gather(phase, own, slot, landed):
        for d in z_order:
            c = copy(own, slot(tok), ag_zs.at[phase, d], ag_zr.at[phase, d], t=zo(d) * R + r)
            c.start()
            pending.append(c)

        def across(src, d, holder):
            for e in range(1, R):
                c = copy(
                    src, slot(holder), ag_ys.at[phase, e, d], ag_yr.at[phase, e, d], t=z * R + ro(e)
                )
                c.start()
                pending.append(c)

        across(own, 0, tok)
        for d in z_wait:
            holder = zo(Z - d) * R + r
            copy(
                slot(holder), slot(holder), ag_zs.at[phase, d], ag_zr.at[phase, d], t=zo(d) * R + r
            ).wait_recv()
            across(slot(holder), d, holder)
            landed(holder)
        for d in [0] + z_wait:
            for e in range(1, R):
                holder = zo(Z - d) * R + ro(R - e)
                copy(
                    slot(holder),
                    slot(holder),
                    ag_ys.at[phase, e, d],
                    ag_yr.at[phase, e, d],
                    t=z * R + ro(e),
                ).wait_recv()
                landed(holder)

    def head_slot(t):
        return heads.at[pl.ds(pl.multiple_of(t * rows, rows), rows)]

    heads[pl.ds(pl.multiple_of(tok * rows, rows), rows), :] = attn_ref[...]
    gather(0, attn_ref, head_slot, lambda holder: None)

    width = out_w_ref.shape[1]
    p = jnp.dot(heads[...], out_w_ref[...], preferred_element_type=jnp.float32)
    proj[...] = p.reshape(T, 2, half_rows, width)
    c = copy(proj.at[:, other], proj_peer, one_s.at[0], one_r.at[0], s=other)
    c.start()
    pending.append(c)
    c.wait_recv()
    cols[...] = (proj[:, side] + proj_peer[...]).astype(jnp.bfloat16)
    for d in range(1, T):
        t = (tok + d) % T
        c = copy(cols.at[t], cols_in.at[tok], col_s.at[d], col_r.at[d], t=t)
        c.start()
        pending.append(c)
    cols_in[tok] = cols[tok]
    for d in range(1, T):
        t = (tok + T - d) % T
        copy(cols.at[t], cols_in.at[t], col_s.at[d], col_r.at[d], t=t).wait_recv()

    my_rows = pl.multiple_of(side * half_rows, half_rows)
    projected = jnp.concatenate([cols_in[t].astype(jnp.float32) for t in range(T)], axis=1)
    low = (hidden_ref[pl.ds(my_rows, half_rows), :].astype(jnp.float32) + projected).astype(
        jnp.bfloat16
    )
    stream_buf[pl.ds(my_rows, half_rows), :] = low
    stream = low.astype(jnp.float32)
    normed = (
        stream
        * lax.rsqrt(jnp.mean(stream * stream, axis=-1, keepdims=True) + 1e-05)
        * gain_ref[...]
    ).astype(jnp.bfloat16)

    def token_slot(t, s=None):
        s = side if s is None else s
        return tokens.at[pl.ds(pl.multiple_of(t * rows + s * half_rows, half_rows), half_rows)]

    tokens[pl.ds(pl.multiple_of(tok * rows + side * half_rows, half_rows), half_rows), :] = normed

    def over(holder):
        c = copy(
            token_slot(holder), token_slot(holder), tok_s.at[holder], tok_r.at[holder], s=other
        )
        c.start()
        pending.append(c)

    expert = z
    lanes = lax.broadcasted_iota(jnp.int32, (1, total), 1)
    block = lax.div(lanes, rows)
    hit = (routes_t_ref[0:1, :] == expert) | (routes_t_ref[1:2, :] == expert)
    row_i = lax.broadcasted_iota(jnp.int32, (total, total), 0)
    col_i = lax.broadcasted_iota(jnp.int32, (total, total), 1)
    before = (row_i < col_i) & (lax.div(row_i, rows) == lax.div(col_i, rows))
    hits = jnp.broadcast_to(jnp.where(hit, 1.0, 0.0), (8, total)).astype(jnp.bfloat16)
    rank = jnp.dot(
        hits,
        jnp.where(before, 1.0, 0.0).astype(jnp.bfloat16),
        preferred_element_type=jnp.float32,
    )[0:1].astype(jnp.int32)
    base = (lax.rem(block, R) * Z + lax.div(block, R)) * cap
    place = jnp.where(hit & (rank < cap), base + rank, -1)
    slot_i = lax.broadcasted_iota(jnp.int32, (slots, total), 0)
    put = jnp.where(slot_i == place, 1.0, 0.0).astype(jnp.bfloat16)

    over(tok)
    c = copy(
        stream_buf.at[pl.ds(my_rows, half_rows)],
        stream_buf.at[pl.ds(my_rows, half_rows)],
        one_s.at[1],
        one_r.at[1],
        s=other,
    )
    c.start()
    pending.append(c)
    gather(1, token_slot(tok), token_slot, over)
    for t in range(T):
        copy(
            token_slot(t, other), token_slot(t, other), tok_s.at[t], tok_r.at[t], s=other
        ).wait_recv()

    @pl.loop(0, D // 512)
    def _(i):
        here = pl.ds(pl.multiple_of(i * 512, 512), 512)
        packed[:, here] = jnp.dot(
            put, tokens[:, here], preferred_element_type=jnp.float32
        ).astype(jnp.bfloat16)

    loads[0].wait()
    loads[1].wait()

    @pl.loop(0, hid // 256)
    def _(i):
        here = pl.ds(pl.multiple_of(i * 256, 256), 256)
        g = jnp.dot(packed[...], gate_w[:, here], preferred_element_type=jnp.float32)
        u = jnp.dot(packed[...], up_w[:, here], preferred_element_type=jnp.float32)
        active[:, here] = (g / (1.0 + jnp.exp(-g)) * u).astype(jnp.bfloat16)

    loads[2].wait()

    @pl.loop(0, half_d // 256)
    def _(i):
        here = pl.ds(pl.multiple_of(i * 256, 256), 256)
        there = pl.ds(pl.multiple_of(other * half_d + i * 256, 256), 256)
        theirs[:, here] = jnp.dot(
            active[...], down_w[:, there], preferred_element_type=jnp.float32
        ).astype(jnp.bfloat16)

    d2d = copy(theirs, theirs_in, one_s.at[2], one_r.at[2], s=other)
    d2d.start()
    pending.append(d2d)

    @pl.loop(0, half_d // 256)
    def _(i):
        here = pl.ds(pl.multiple_of(i * 256, 256), 256)
        there = pl.ds(pl.multiple_of(side * half_d + i * 256, 256), 256)
        mine[:, here] = jnp.dot(active[...], down_w[:, there], preferred_element_type=jnp.float32)

    d2d.wait_recv()
    mine[...] = mine[...] + theirs_in[...].astype(jnp.float32)

    back = z_order + [0]
    for d in back:
        for e in range(1, R):
            at = pl.multiple_of(ro(e) * part + zo(d) * cap, 8)
            y_out[e, d] = wire(mine[pl.ds(at, cap), :])
            c = copy(y_out.at[e, d], y_in.at[e, d], ry_s.at[e, d], ry_r.at[e, d], t=z * R + ro(e))
            c.start()
            pending.append(c)
    for d in back:
        at = pl.multiple_of(r * part + zo(d) * cap, 8)
        total_rows = mine[pl.ds(at, cap), :]
        for e in range(1, R):
            copy(
                y_out.at[e, d], y_in.at[e, d], ry_s.at[e, d], ry_r.at[e, d], t=z * R + ro(e)
            ).wait_recv()
            total_rows = total_rows + unwire(y_in[e, d], half_d)
        if d == 0:
            z_in[z] = wire(total_rows)
        else:
            z_out[d] = wire(total_rows)
            c = copy(z_out.at[d], z_in.at[z], rz_s.at[d], rz_r.at[d], t=zo(d) * R + r)
            c.start()
            pending.append(c)

    own = pl.ds(pl.multiple_of(tok * rows, rows), rows)
    logits = jnp.dot(tokens[own, :], router_ref[...], preferred_element_type=jnp.float32)
    chosen = routes_ref[own, :]
    r0, r1 = chosen[:, 0:1], chosen[:, 1:2]
    lane = lax.broadcasted_iota(jnp.int32, (rows, 128), 1)

    def parts(k):
        return (lane == k) | (lane == k + Z) | (lane == k + 2 * Z)

    l0 = jnp.sum(jnp.where(parts(r0), logits, 0.0), axis=1, keepdims=True)
    l1 = jnp.sum(jnp.where(parts(r1), logits, 0.0), axis=1, keepdims=True)
    g0 = 1.0 / (1.0 + jnp.exp(l1 - l0))
    g1 = 1.0 - g0
    both = jnp.where((lane == r0) | (lane == r1), 1.0, 0.0).astype(jnp.bfloat16)
    row_n = lax.broadcasted_iota(jnp.int32, (rows, rows), 0)
    col_n = lax.broadcasted_iota(jnp.int32, (rows, rows), 1)
    ranks = jnp.dot(
        jnp.where(col_n < row_n, 1.0, 0.0).astype(jnp.bfloat16),
        both,
        preferred_element_type=jnp.float32,
    ).astype(jnp.int32)
    at = lax.broadcasted_iota(jnp.int32, (rows, part), 1)

    def find(k):
        rank = jnp.sum(jnp.where(lane == k, ranks, 0), axis=1, keepdims=True)
        return jnp.where(at == k * cap + rank, 1.0, 0.0).astype(jnp.bfloat16)

    pick0, pick1 = find(r0), find(r1)

    copy(
        stream_buf.at[pl.ds(my_rows, half_rows)],
        stream_buf.at[pl.ds(pl.multiple_of(other * half_rows, half_rows), half_rows)],
        one_s.at[1],
        one_r.at[1],
        s=other,
    ).wait_recv()
    for d in z_wait:
        src = zo(Z - d)
        copy(z_out.at[d], z_in.at[src], rz_s.at[d], rz_r.at[d], t=zo(d) * R + r).wait_recv()
    got = jnp.concatenate([unwire(z_in[e], half_d) for e in range(Z)], axis=0).astype(jnp.bfloat16)
    half = pl.ds(pl.multiple_of(side * half_d, half_d), half_d)
    mixed = (
        stream_buf[:, half].astype(jnp.float32)
        + g0 * jnp.dot(pick0, got, preferred_element_type=jnp.float32)
        + g1 * jnp.dot(pick1, got, preferred_element_type=jnp.float32)
    )
    final[side] = mixed.astype(jnp.bfloat16)
    c = copy(final.at[side], final.at[side], one_s.at[3], one_r.at[3], s=other)
    c.start()
    pending.append(c)
    copy(final.at[other], final.at[other], one_s.at[3], one_r.at[3], s=other).wait_recv()
    out_ref[:, :half_d] = final[0]
    out_ref[:, half_d:] = final[1]
    for c in pending:
        c.wait_send()


def local(
    hidden_in,
    queries,
    key_new,
    value_new,
    cache_keys,
    cache_values,
    lengths,
    out_weight,
    norm_gain,
    router_weight,
    gate_weight,
    up_weight,
    down_weight,
    routes,
):
    rows, D = hidden_in.shape
    T = lax.axis_size("tok")
    Z = router_weight.shape[1]
    R = T // Z
    cap = min(CAP, rows)
    hid = gate_weight.shape[1]
    width = out_weight.shape[1]
    bf, f32 = jnp.bfloat16, jnp.float32
    attn_out = attend(queries, key_new, value_new, cache_keys, cache_values, lengths)
    first = lax.reduce_precision(router_weight, 8, 7)
    second = lax.reduce_precision(router_weight - first, 8, 7)
    third = router_weight - first - second
    router = jnp.concatenate(
        [first, second, third, jnp.zeros((D, 128 - 3 * Z), f32)], axis=1
    ).astype(bf)
    half_d = D // 2
    wire_width = half_d * cap // 16
    dma = pltpu.SemaphoreType.DMA
    vmem = pl.BlockSpec(memory_space=pltpu.VMEM)
    anyspace = pl.BlockSpec(memory_space=pl.ANY)
    return pl.pallas_call(
        functools.partial(body, (T, Z, R, rows, cap)),
        out_shape=jax.ShapeDtypeStruct((rows, D), bf),
        in_specs=[vmem] * 7 + [anyspace] * 3,
        out_specs=vmem,
        scratch_shapes=[
            pltpu.VMEM((T * rows, attn_out.shape[1]), bf),
            pltpu.VMEM((T, 2, rows // 2, width), f32),
            pltpu.VMEM((T, rows // 2, width), f32),
            pltpu.VMEM((T, rows // 2, width), bf),
            pltpu.VMEM((T, rows // 2, width), bf),
            pltpu.VMEM((rows, D), bf),
            pltpu.VMEM((T * rows, D), bf),
            pltpu.VMEM((T * cap, D), bf),
            pltpu.VMEM((T * cap, hid), bf),
            pltpu.VMEM(gate_weight.shape, bf),
            pltpu.VMEM(up_weight.shape, bf),
            pltpu.VMEM(down_weight.shape, bf),
            pltpu.VMEM((T * cap, half_d), f32),
            pltpu.VMEM((T * cap, half_d), bf),
            pltpu.VMEM((T * cap, half_d), bf),
            pltpu.VMEM((R, Z, 16, wire_width), bf),
            pltpu.VMEM((R, Z, 16, wire_width), bf),
            pltpu.VMEM((Z, 16, wire_width), bf),
            pltpu.VMEM((Z, 16, wire_width), bf),
            pltpu.VMEM((2, rows, half_d), bf),
            dma((3,)),
            dma((2, Z)),
            dma((2, Z)),
            dma((2, R, Z)),
            dma((2, R, Z)),
            dma((T,)),
            dma((T,)),
            dma((T,)),
            dma((T,)),
            dma((4,)),
            dma((4,)),
            dma((Z,)),
            dma((Z,)),
            dma((R, Z)),
            dma((R, Z)),
        ],
        compiler_params=pltpu.CompilerParams(
            collective_id=0, has_side_effects=True, vmem_limit_bytes=67043328
        ),
    )(
        attn_out,
        hidden_in,
        routes,
        routes.T,
        norm_gain.reshape(1, D),
        router,
        out_weight,
        gate_weight,
        up_weight,
        down_weight,
    )


def solution(mesh):
    return jax.shard_map(
        local,
        mesh=mesh,
        in_specs=(
            P(("grp", "tok"), None),
            P(("grp", "tok"), "side", None),
            P(("grp", "tok"), "side", None),
            P(("grp", "tok"), "side", None),
            P(("grp", "tok"), "side", None, None),
            P(("grp", "tok"), "side", None, None),
            P(("grp", "tok")),
            P("side", "tok"),
            P(),
            P(),
            P(None, ("tok", "side")),
            P(None, ("tok", "side")),
            P(("tok", "side"), None),
            P("grp", None),
        ),
        out_specs=P(("grp", "tok"), None),
        check_vma=False,
    )
```

time: 226 us -> 90.8 us (0.40)
  blocking collectives: 141 us -> 0 us
  Pallas kernels: 0 us -> 76.1 us
  waiting for transfers between devices: 34.4 us -> 0 us
  matrix products: 30.5 us -> 4 us
  between operations: 13.6 us -> 0.12 us
  local copies, waits for them, and re-layouts: 1.31 us -> 4.71 us
    all_to_all x3 -> x0, blocking collectives: 107 us -> none  [the longest x1 57 us: local(): lax.all_to_all(partial_rows.reshape(sources, slots, width_in), 'tok', spl...]
    pallas_call x0 -> x1, Pallas kernels: none -> 76.1 us  [local(): pl.pallas_call(functools.partial(body, (T, Z, R, rows, cap)), out_shape=j...]
    psum x2 -> x0, waiting for transfers between devices: 34.4 us -> none  [the longest x1 17.5 us: local(): combined_all = lax.psum(combined, 'side')]
    all_gather x1 -> x0, blocking collectives: 33.8 us -> none  [local(): lax.all_gather(attn_out, 'tok', axis=0, tiled=True)]
    dot_general x6 -> x0, matrix products: 26.4 us -> none  [the longest x1 15.3 us: expert_rows(): return jnp.dot(active, down_weight, preferred_element_type=jnp.float32)]
    concatenate x0 -> x1, other arithmetic: none -> 3.04 us  [local(): jnp.concatenate([first, second, third, jnp.zeros((D, 128 - 3 * Z), f32)],...]
    unnamed x14 -> x15, local copies, waits for them, and re-layouts: 0.04 us -> 2.95 us
  transfers between devices with their start and end apart: 2 -> 0, of which waited for: 2 -> 0; matrix products, arithmetic and copies ran while one was open for 0% -> 0% of each run, Pallas kernels for 0% -> 0%
where the time goes in v1:
time: 90.8 us; the launch traced here: 90.6 us
  Pallas kernels  76.1 us (84%)
  other arithmetic  5.65 us (6%)
  local copies, waits for them, and re-layouts  4.71 us (5%)
  matrix products  4 us (4%)
    pallas_call x1, Pallas kernels, local(): pl.pallas_call(functools.partial(body, (T, Z, R, rows, cap)), out_shape=j...  76.1 us
    dot_general x1, matrix products, attend(): jnp.einsum('skgd,skpd->skgp', grouped, cache_keys, preferred_element_type...  3.08 us
    concatenate x1, other arithmetic, local(): jnp.concatenate([first, second, third, jnp.zeros((D, 128 - 3 * Z), f32)],...  3.04 us
    unnamed x15, local copies, waits for them, and re-layouts  2.95 us

profile of v1, /device:TPU:0, one launch (start us, length us, event | category | flops | bytes accessed | tf_op | source)
XLA Modules:
  0.0 90.6 jit_solution(8751041073683208643)
XLA Ops:
  0.0 0.0 copy-start.1
  0.0 0.0 copy-start.5
  0.0 0.8 iota_compare_fusion
  0.8 0.0 copy-start.2
  0.8 0.0 copy-start.4
  0.8 3.1 %fusion.12 = (f32[32,2,6]{2,1,0:T(2,128)S(1)}, f32[32,2,6,128]{3,2,1,0:T(8,128)S(1)}) fusion(bf16[32,2,128,128]{3,2,1,0:T(8,128)(2,1)} %param.18, bf16[32,2,6,128]{3,0,2,1:T(8,128)(2,1)} %bitcast.8, pred[32,128]{1,0:T(8,128)(4,1)S(1)} %iota_compare_fusion), kind=kOutput, calls=%fused_computation.24 | convolution fusion | flops 12729984 | bytes 2397696 | tf_op jit(solution)/shard_map/skgd,skpd->skgp/dot_general | solution.py:21
  3.9 0.0 copy-done.1
  3.9 0.0 copy-done.5
  3.9 0.2 fusion.4
  4.1 0.3 fusion.3
  4.4 0.1 fusion.11
  4.5 0.0 copy-done.2
  4.5 0.0 copy-done.4
  4.5 0.0 copy-start
  4.5 0.7 fusion.2
  5.2 0.8 reshape.31.attn_ref
  6.0 0.0 copy-done
  6.0 0.5 copy.25
  6.5 0.5 copy.24
  7.0 1.5 %reduce-precision_convert_fusion = (bf16[3072,4]{1,0:T(8,128)(2,1)}, bf16[3072,4]{1,0:T(8,128)(2,1)}) fusion(f32[3072,4]{1,0:T(8,128)S(1)} %copy.24, f32[3072,4]{1,0:T(8,128)S(1)} %copy.25), kind=kLoop, calls=%fused_computation.1 | loop fusion | flops 61440 | bytes 147456 | tf_op jit(solution)/shard_map/convert.1
  8.5 0.4 copy.26
  8.9 0.1 pad.3.clone
  9.0 0.0 copy-start.3
  9.0 3.0 %maximum_maximum_fusion.router_ref = bf16[3072,128]{1,0:T(8,128)(2,1)} fusion(bf16[3072,4]{1,0:T(8,128)(2,1)} %get-tuple-element.6, bf16[3072,4]{1,0:T(8,128)(2,1)} %get-tuple-element.5, bf16[3072,4]{1,0:T(8,128)(2,1)S(1)} %copy.26, bf16[128]{0:T(256)(128)(2,1)S(1)} %pad.3.clone), kind=kLoop, calls=%fused_computation.7 | loop fusion | flops 3145728 | bytes 860416 | tf_op jit(solution)/shard_map/concatenate | solution.py:431
  12.1 0.0 copy-done.3
  12.1 0.8 copy.27.routes_ref
  12.9 76.1 %shard_map.136 = bf16[32,3072]{1,0:T(8,128)(2,1)} custom-call(bf16[32,1536]{1,0:T(8,128)(2,1)} %reshape.31.attn_ref, bf16[32,3072]{1,0:T(8,128)(2,1)} %hidden_ref.1, s32[256,2]{1,0:T(8,128)} %copy.27.routes_ref, s32[2,256]{1,0:T(2,128)} %bitcast.13, f32[1,3072]{1,0:T(1,128)} %bitcast.12, bf16[3072,128]{1,0:T(8,128)(2,1)} %maximum_maximum_fusion.router_ref, ...), custom_call_target="tpu_custom_call" | custom-call | tf_op jit(solution)/shard_map/pallas_call | solution.py:439
  88.9 1.6 %copy.39 = bf16[32,3072]{1,0:T(8,128)(2,1)} copy(bf16[32,3072]{1,0:T(8,128)(2,1)} %shard_map.136) | data formatting | bytes 393216
  (4 shorter events, 0.1 us)
Async XLA Ops:
  0.0 3.9 %copy-start.1 = (bf16[32,12,128]{2,0,1:T(8,128)(2,1)S(1)}, bf16[32,12,128]{2,0,1:T(8,128)(2,1)}, u32[]{:S(2)}) copy-start(bf16[32,12,128]{2,0,1:T(8,128)(2,1)} %param.15) | copy-start | bytes 294916
  0.0 3.9 %copy-start.5 = (bf16[32,2,128]{2,1,0:T(2,128)(2,1)S(1)}, bf16[32,2,128]{2,1,0:T(2,128)(2,1)}, u32[]{:S(2)}) copy-start(bf16[32,2,128]{2,1,0:T(2,128)(2,1)} %param.16) | copy-start | bytes 49156
  0.8 3.7 %copy-start.2 = (bf16[32,2,128]{2,1,0:T(2,128)(2,1)S(1)}, bf16[32,2,128]{2,1,0:T(2,128)(2,1)}, u32[]{:S(2)}) copy-start(bf16[32,2,128]{2,1,0:T(2,128)(2,1)} %param.17) | copy-start | bytes 49156
  0.8 3.7 %copy-start.4 = (bf16[32,2,128,128]{3,2,1,0:T(8,128)(2,1)S(1)}, bf16[32,2,128,128]{3,2,1,0:T(8,128)(2,1)}, u32[]{:S(2)}) copy-start(bf16[32,2,128,128]{3,2,1,0:T(8,128)(2,1)} %param.19) | copy-start | bytes 6291460
  4.5 1.5 %copy-start = (f32[3072,4]{0,1:T(4,128)S(1)}, f32[3072,4]{0,1:T(4,128)}, u32[]{:S(2)}) copy-start(f32[3072,4]{0,1:T(4,128)} %param.23) | copy-start | bytes 147460
  9.0 3.0 %copy-start.3 = (s32[256,2]{0,1:T(2,128)S(1)}, s32[256,2]{0,1:T(2,128)}, u32[]{:S(2)}) copy-start(s32[256,2]{0,1:T(2,128)} %param.27) | copy-start | bytes 6148

commit v2 on v1

--- a/solution.py
+++ b/solution.py
@@ -9,6 +9,9 @@
 from jax.sharding import PartitionSpec as P
 
 CAP = 24
+PIECES = 4
+HIDDEN_TILE = 512
+STRIPS = 2
 
 
 def attend(queries, key_new, value_new, cache_keys, cache_values, lengths):
@@ -60,11 +63,10 @@
     dims,
     attn_ref,
     hidden_ref,
-    routes_ref,
     routes_t_ref,
     gain_ref,
     router_ref,
-    out_w_ref,
+    out_hbm,
     gate_hbm,
     up_hbm,
     down_hbm,
@@ -78,6 +80,7 @@
     tokens,
     packed,
     active,
+    out_w,
     gate_w,
     up_w,
     down_w,
@@ -137,6 +140,7 @@
         )
 
     loads = [
+        pltpu.make_async_copy(out_hbm, out_w, w_sem.at[3]),
         pltpu.make_async_copy(gate_hbm, gate_w, w_sem.at[0]),
         pltpu.make_async_copy(up_hbm, up_w, w_sem.at[1]),
         pltpu.make_async_copy(down_hbm, down_w, w_sem.at[2]),
@@ -144,6 +148,7 @@
     for load in loads:
         load.start()
 
+    heads[pl.ds(pl.multiple_of(tok * rows, rows), rows), :] = attn_ref[...]
     barrier = pltpu.get_barrier_semaphore()
     for d in range(1, T):
         pl.semaphore_signal(
@@ -157,52 +162,108 @@
     )
     pl.semaphore_wait(barrier, T)
 
-    z_order = sorted(range(1, Z), key=lambda d: -min(d, Z - d))
-    z_wait = z_order[::-1]
     pending = []
 
-    def gather(phase, own, slot, landed):
-        for d in z_order:
-            c = copy(own, slot(tok), ag_zs.at[phase, d], ag_zr.at[phase, d], t=zo(d) * R + r)
-            c.start()
-            pending.append(c)
-
-        def across(src, d, holder):
+    def gather(phase, slot, landed):
+        def along(zs, hop, way, piece):
+            k = (phase, hop, (way + 1) // 2, piece)
+            here = slot(zs * R + r, piece)
+            return copy(here, here, ag_zs.at[k], ag_zr.at[k], t=(z + way) * R + r)
+
+        def landing(zs, hop, way, piece):
+            k = (phase, hop, (way + 1) // 2, piece)
+            here = slot(zs * R + r, piece)
+            return copy(here, here, ag_zs.at[k], ag_zr.at[k], t=tok)
+
+        def across(zs, piece):
             for e in range(1, R):
-                c = copy(
-                    src, slot(holder), ag_ys.at[phase, e, d], ag_yr.at[phase, e, d], t=z * R + ro(e)
-                )
+                k = (phase, e, zs, piece)
+                here = slot(zs * R + r, piece)
+                c = copy(here, here, ag_ys.at[k], ag_yr.at[k], t=z * R + ro(e))
                 c.start()
-                pending.append(c)
-
-        across(own, 0, tok)
-        for d in z_wait:
-            holder = zo(Z - d) * R + r
-            copy(
-                slot(holder), slot(holder), ag_zs.at[phase, d], ag_zr.at[phase, d], t=zo(d) * R + r
-            ).wait_recv()
-            across(slot(holder), d, holder)
-            landed(holder)
-        for d in [0] + z_wait:
+
+        def crossed(zs, piece):
             for e in range(1, R):
-                holder = zo(Z - d) * R + ro(R - e)
-                copy(
-                    slot(holder),
-                    slot(holder),
-                    ag_ys.at[phase, e, d],
-                    ag_yr.at[phase, e, d],
-                    t=z * R + ro(e),
-                ).wait_recv()
-                landed(holder)
-
-    def head_slot(t):
-        return heads.at[pl.ds(pl.multiple_of(t * rows, rows), rows)]
-
-    heads[pl.ds(pl.multiple_of(tok * rows, rows), rows), :] = attn_ref[...]
-    gather(0, attn_ref, head_slot, lambda holder: None)
-
-    width = out_w_ref.shape[1]
-    p = jnp.dot(heads[...], out_w_ref[...], preferred_element_type=jnp.float32)
+                k = (phase, e, zs, piece)
+                here = slot(zs * R + ro(R - e), piece)
+                copy(here, here, ag_ys.at[k], ag_yr.at[k], t=z * R + ro(e)).wait_recv()
+                landed(zs * R + ro(R - e), piece)
+
+        def send_on(zs, hop, way, piece):
+            ok = (z + way >= 0) & (z + way < Z)
+
+            @pl.when(ok)
+            def _():
+                along(zs, hop, way, piece).start()
+
+        for piece in range(PIECES):
+            for way in (1, -1):
+                send_on(z, 0, way, piece)
+            across(z, piece)
+        for hop in range(1, Z):
+            for piece in range(PIECES):
+                for way in (1, -1):
+                    zs = z - way * hop
+
+                    @pl.when((zs >= 0) & (zs < Z))
+                    def _(zs=zs, way=way, piece=piece, hop=hop):
+                        landing(zs, hop - 1, way, piece).wait_recv()
+                        if hop < Z - 1:
+                            send_on(zs, hop, way, piece)
+                        across(zs, piece)
+                        landed(zs * R + r, piece)
+
+            for piece in range(PIECES):
+                if hop == 1:
+                    crossed(z, piece)
+                else:
+                    for way in (1, -1):
+                        zs = z - way * (hop - 1)
+
+                        @pl.when((zs >= 0) & (zs < Z))
+                        def _(zs=zs, piece=piece):
+                            crossed(zs, piece)
+
+        for piece in range(PIECES):
+            for way in (1, -1):
+                zs = z - way * (Z - 1)
+
+                @pl.when((zs >= 0) & (zs < Z))
+                def _(zs=zs, piece=piece):
+                    crossed(zs, piece)
+
+    def settle(phase, slot):
+        for piece in range(PIECES):
+            for zs in range(Z):
+                for e in range(1, R):
+                    k = (phase, e, zs, piece)
+                    here = slot(zs * R + r, piece)
+                    copy(here, here, ag_ys.at[k], ag_yr.at[k], t=z * R + ro(e)).wait_send()
+            for hop in range(Z - 1):
+                for way in (1, -1):
+                    zs = z - way * hop
+                    ok = (zs >= 0) & (zs < Z) & (z + way >= 0) & (z + way < Z)
+
+                    @pl.when(ok)
+                    def _(zs=zs, hop=hop, way=way, piece=piece):
+                        k = (phase, hop, (way + 1) // 2, piece)
+                        here = slot(zs * R + r, piece)
+                        copy(
+                            here, here, ag_zs.at[k], ag_zr.at[k], t=(z + way) * R + r
+                        ).wait_send()
+
+    head_piece = heads.shape[1] // PIECES
+
+    def head_slot(t, piece):
+        return heads.at[
+            pl.ds(pl.multiple_of(t * rows, rows), rows), pl.ds(piece * head_piece, head_piece)
+        ]
+
+    gather(0, head_slot, lambda holder, piece: None)
+    loads[0].wait()
+
+    width = out_w.shape[1]
+    p = jnp.dot(heads[...], out_w[...], preferred_element_type=jnp.float32)
     proj[...] = p.reshape(T, 2, half_rows, width)
     c = copy(proj.at[:, other], proj_peer, one_s.at[0], one_r.at[0], s=other)
     c.start()
@@ -232,18 +293,20 @@
         * gain_ref[...]
     ).astype(jnp.bfloat16)
 
-    def token_slot(t, s=None):
+    token_piece = D // PIECES
+
+    def token_slot(t, piece, s=None):
         s = side if s is None else s
-        return tokens.at[pl.ds(pl.multiple_of(t * rows + s * half_rows, half_rows), half_rows)]
+        return tokens.at[
+            pl.ds(pl.multiple_of(t * rows + s * half_rows, half_rows), half_rows),
+            pl.ds(piece * token_piece, token_piece),
+        ]
 
     tokens[pl.ds(pl.multiple_of(tok * rows + side * half_rows, half_rows), half_rows), :] = normed
 
-    def over(holder):
-        c = copy(
-            token_slot(holder), token_slot(holder), tok_s.at[holder], tok_r.at[holder], s=other
-        )
-        c.start()
-        pending.append(c)
+    def over(holder, piece, s=None):
+        here = token_slot(holder, piece, s)
+        return copy(here, here, tok_s.at[holder, piece], tok_r.at[holder, piece], s=other)
 
     expert = z
     lanes = lax.broadcasted_iota(jnp.int32, (1, total), 1)
@@ -263,7 +326,8 @@
     slot_i = lax.broadcasted_iota(jnp.int32, (slots, total), 0)
     put = jnp.where(slot_i == place, 1.0, 0.0).astype(jnp.bfloat16)
 
-    over(tok)
+    for piece in range(PIECES):
+        over(tok, piece).start()
     c = copy(
         stream_buf.at[pl.ds(my_rows, half_rows)],
         stream_buf.at[pl.ds(my_rows, half_rows)],
@@ -273,11 +337,10 @@
     )
     c.start()
     pending.append(c)
-    gather(1, token_slot(tok), token_slot, over)
+    gather(1, token_slot, lambda holder, piece: over(holder, piece).start())
     for t in range(T):
-        copy(
-            token_slot(t, other), token_slot(t, other), tok_s.at[t], tok_r.at[t], s=other
-        ).wait_recv()
+        for piece in range(PIECES):
+            over(t, piece, other).wait_recv()
 
     @pl.loop(0, D // 512)
     def _(i):
@@ -286,74 +349,83 @@
             put, tokens[:, here], preferred_element_type=jnp.float32
         ).astype(jnp.bfloat16)
 
-    loads[0].wait()
     loads[1].wait()
-
-    @pl.loop(0, hid // 256)
+    loads[2].wait()
+
+    tile = min(HIDDEN_TILE, hid)
+
+    @pl.loop(0, hid // tile)
     def _(i):
-        here = pl.ds(pl.multiple_of(i * 256, 256), 256)
+        here = pl.ds(pl.multiple_of(i * tile, tile), tile)
         g = jnp.dot(packed[...], gate_w[:, here], preferred_element_type=jnp.float32)
         u = jnp.dot(packed[...], up_w[:, here], preferred_element_type=jnp.float32)
         active[:, here] = (g / (1.0 + jnp.exp(-g)) * u).astype(jnp.bfloat16)
 
-    loads[2].wait()
-
-    @pl.loop(0, half_d // 256)
-    def _(i):
-        here = pl.ds(pl.multiple_of(i * 256, 256), 256)
-        there = pl.ds(pl.multiple_of(other * half_d + i * 256, 256), 256)
-        theirs[:, here] = jnp.dot(
-            active[...], down_w[:, there], preferred_element_type=jnp.float32
-        ).astype(jnp.bfloat16)
-
-    d2d = copy(theirs, theirs_in, one_s.at[2], one_r.at[2], s=other)
-    d2d.start()
-    pending.append(d2d)
-
-    @pl.loop(0, half_d // 256)
-    def _(i):
-        here = pl.ds(pl.multiple_of(i * 256, 256), 256)
-        there = pl.ds(pl.multiple_of(side * half_d + i * 256, 256), 256)
-        mine[:, here] = jnp.dot(active[...], down_w[:, there], preferred_element_type=jnp.float32)
-
-    d2d.wait_recv()
-    mine[...] = mine[...] + theirs_in[...].astype(jnp.float32)
-
-    back = z_order + [0]
-    for d in back:
-        for e in range(1, R):
-            at = pl.multiple_of(ro(e) * part + zo(d) * cap, 8)
-            y_out[e, d] = wire(mine[pl.ds(at, cap), :])
-            c = copy(y_out.at[e, d], y_in.at[e, d], ry_s.at[e, d], ry_r.at[e, d], t=z * R + ro(e))
-            c.start()
-            pending.append(c)
-    for d in back:
-        at = pl.multiple_of(r * part + zo(d) * cap, 8)
-        total_rows = mine[pl.ds(at, cap), :]
-        for e in range(1, R):
-            copy(
-                y_out.at[e, d], y_in.at[e, d], ry_s.at[e, d], ry_r.at[e, d], t=z * R + ro(e)
-            ).wait_recv()
-            total_rows = total_rows + unwire(y_in[e, d], half_d)
-        if d == 0:
-            z_in[z] = wire(total_rows)
-        else:
-            z_out[d] = wire(total_rows)
-            c = copy(z_out.at[d], z_in.at[z], rz_s.at[d], rz_r.at[d], t=zo(d) * R + r)
-            c.start()
-            pending.append(c)
+    loads[3].wait()
+
+    strip = half_d // STRIPS
+    far_up = z < Z // 2
+
+    def down(start, q):
+        at = pl.ds(pl.multiple_of(start * half_d + q * strip, 128), strip)
+        return jnp.dot(active[...], down_w[:, at], preferred_element_type=jnp.float32)
+
+    def y_copy(q, e, k):
+        i = (q, e, k)
+        return copy(y_out.at[i], y_in.at[i], ry_s.at[i], ry_r.at[i], t=z * R + ro(e))
+
+    def cores_copy(q):
+        return copy(theirs.at[q], theirs_in.at[q], one_s.at[q + 4], one_r.at[q + 4], s=other)
+
+    for q in range(STRIPS):
+        theirs[q] = down(other, q).astype(jnp.bfloat16)
+        cores_copy(q).start()
+        mine[q] = down(side, q)
+        cores_copy(q).wait_recv()
+        mine[q] = mine[q] + theirs_in[q].astype(jnp.float32)
+        for k in range(Z):
+            to = jnp.where(far_up, Z - 1 - k, k)
+            for e in range(1, R):
+                at = pl.multiple_of(ro(e) * part + to * cap, 8)
+                y_out[q, e, k] = wire(mine[q, pl.ds(at, cap), :])
+                y_copy(q, e, k).start()
+    for q in range(STRIPS):
+        for k in range(Z):
+            to = jnp.where(far_up, Z - 1 - k, k)
+            at = pl.multiple_of(r * part + to * cap, 8)
+            total_rows = mine[q, pl.ds(at, cap), :]
+            for e in range(1, R):
+                y_copy(q, e, k).wait_recv()
+                total_rows = total_rows + unwire(y_in[q, e, k], strip)
+            z_out[q, to] = wire(total_rows)
+
+            @pl.when(to == z)
+            def _(to=to, q=q):
+                z_in[q, z] = z_out[q, to]
+
+            @pl.when(to != z)
+            def _(to=to, q=q):
+                copy(
+                    z_out.at[q, to], z_in.at[q, z], rz_s.at[q, to], rz_r.at[q, z], t=to * R + r
+                ).start()
 
     own = pl.ds(pl.multiple_of(tok * rows, rows), rows)
-    logits = jnp.dot(tokens[own, :], router_ref[...], preferred_element_type=jnp.float32)
-    chosen = routes_ref[own, :]
-    r0, r1 = chosen[:, 0:1], chosen[:, 1:2]
+    mine_now = tokens[own, :].astype(jnp.float32)
+    lane_t = lax.broadcasted_iota(jnp.int32, (rows, total), 1)
+    row_t = lax.broadcasted_iota(jnp.int32, (rows, total), 0)
+    at_own = lane_t == tok * rows + row_t
+
+    def own_route(k):
+        return jnp.sum(jnp.where(at_own, routes_t_ref[k : k + 1, :], 0), axis=1, keepdims=True)
+
+    r0, r1 = own_route(0), own_route(1)
     lane = lax.broadcasted_iota(jnp.int32, (rows, 128), 1)
-
-    def parts(k):
-        return (lane == k) | (lane == k + Z) | (lane == k + 2 * Z)
-
-    l0 = jnp.sum(jnp.where(parts(r0), logits, 0.0), axis=1, keepdims=True)
-    l1 = jnp.sum(jnp.where(parts(r1), logits, 0.0), axis=1, keepdims=True)
+    l0 = jnp.zeros((rows, 1), jnp.float32)
+    l1 = jnp.zeros((rows, 1), jnp.float32)
+    for k in range(Z):
+        logit = jnp.sum(mine_now * router_ref[k : k + 1, :], axis=1, keepdims=True)
+        l0 = jnp.where(r0 == k, logit, l0)
+        l1 = jnp.where(r1 == k, logit, l1)
     g0 = 1.0 / (1.0 + jnp.exp(l1 - l0))
     g1 = 1.0 - g0
     both = jnp.where((lane == r0) | (lane == r1), 1.0, 0.0).astype(jnp.bfloat16)
@@ -379,16 +451,20 @@
         one_r.at[1],
         s=other,
     ).wait_recv()
-    for d in z_wait:
-        src = zo(Z - d)
-        copy(z_out.at[d], z_in.at[src], rz_s.at[d], rz_r.at[d], t=zo(d) * R + r).wait_recv()
-    got = jnp.concatenate([unwire(z_in[e], half_d) for e in range(Z)], axis=0).astype(jnp.bfloat16)
+    strips = []
+    for q in range(STRIPS):
+        for d in range(1, Z):
+            src = zo(d)
+            here = z_in.at[q, src]
+            copy(here, here, rz_s.at[q, src], rz_r.at[q, src], t=src * R + r).wait_recv()
+        got = jnp.concatenate([unwire(z_in[q, e], strip) for e in range(Z)], axis=0)
+        got = got.astype(jnp.bfloat16)
+        strips.append(
+            g0 * jnp.dot(pick0, got, preferred_element_type=jnp.float32)
+            + g1 * jnp.dot(pick1, got, preferred_element_type=jnp.float32)
+        )
     half = pl.ds(pl.multiple_of(side * half_d, half_d), half_d)
-    mixed = (
-        stream_buf[:, half].astype(jnp.float32)
-        + g0 * jnp.dot(pick0, got, preferred_element_type=jnp.float32)
-        + g1 * jnp.dot(pick1, got, preferred_element_type=jnp.float32)
-    )
+    mixed = stream_buf[:, half].astype(jnp.float32) + jnp.concatenate(strips, axis=1)
     final[side] = mixed.astype(jnp.bfloat16)
     c = copy(final.at[side], final.at[side], one_s.at[3], one_r.at[3], s=other)
     c.start()
@@ -398,6 +474,21 @@
     out_ref[:, half_d:] = final[1]
     for c in pending:
         c.wait_send()
+    for q in range(STRIPS):
+        cores_copy(q).wait_send()
+        for e in range(1, R):
+            for k in range(Z):
+                y_copy(q, e, k).wait_send()
+        for d in range(1, Z):
+            to = zo(d)
+            copy(
+                z_out.at[q, to], z_in.at[q, z], rz_s.at[q, to], rz_r.at[q, z], t=to * R + r
+            ).wait_send()
+    settle(0, head_slot)
+    settle(1, token_slot)
+    for t in range(T):
+        for piece in range(PIECES):
+            over(t, piece).wait_send()
 
 
 def local(
@@ -425,21 +516,16 @@
     width = out_weight.shape[1]
     bf, f32 = jnp.bfloat16, jnp.float32
     attn_out = attend(queries, key_new, value_new, cache_keys, cache_values, lengths)
-    first = lax.reduce_precision(router_weight, 8, 7)
-    second = lax.reduce_precision(router_weight - first, 8, 7)
-    third = router_weight - first - second
-    router = jnp.concatenate(
-        [first, second, third, jnp.zeros((D, 128 - 3 * Z), f32)], axis=1
-    ).astype(bf)
     half_d = D // 2
-    wire_width = half_d * cap // 16
+    strip = half_d // STRIPS
+    wire_width = strip * cap // 16
     dma = pltpu.SemaphoreType.DMA
     vmem = pl.BlockSpec(memory_space=pltpu.VMEM)
     anyspace = pl.BlockSpec(memory_space=pl.ANY)
     return pl.pallas_call(
         functools.partial(body, (T, Z, R, rows, cap)),
         out_shape=jax.ShapeDtypeStruct((rows, D), bf),
-        in_specs=[vmem] * 7 + [anyspace] * 3,
+        in_specs=[vmem] * 5 + [anyspace] * 4,
         out_specs=vmem,
         scratch_shapes=[
             pltpu.VMEM((T * rows, attn_out.shape[1]), bf),
@@ -451,32 +537,33 @@
             pltpu.VMEM((T * rows, D), bf),
             pltpu.VMEM((T * cap, D), bf),
             pltpu.VMEM((T * cap, hid), bf),
+            pltpu.VMEM(out_weight.shape, bf),
             pltpu.VMEM(gate_weight.shape, bf),
             pltpu.VMEM(up_weight.shape, bf),
             pltpu.VMEM(down_weight.shape, bf),
-            pltpu.VMEM((T * cap, half_d), f32),
-            pltpu.VMEM((T * cap, half_d), bf),
-            pltpu.VMEM((T * cap, half_d), bf),
-            pltpu.VMEM((R, Z, 16, wire_width), bf),
-            pltpu.VMEM((R, Z, 16, wire_width), bf),
-            pltpu.VMEM((Z, 16, wire_width), bf),
-            pltpu.VMEM((Z, 16, wire_width), bf),
+            pltpu.VMEM((STRIPS, T * cap, strip), f32),
+            pltpu.VMEM((STRIPS, T * cap, strip), bf),
+            pltpu.VMEM((STRIPS, T * cap, strip), bf),
+            pltpu.VMEM((STRIPS, R, Z, 16, wire_width), bf),
+            pltpu.VMEM((STRIPS, R, Z, 16, wire_width), bf),
+            pltpu.VMEM((STRIPS, Z, 16, wire_width), bf),
+            pltpu.VMEM((STRIPS, Z, 16, wire_width), bf),
             pltpu.VMEM((2, rows, half_d), bf),
-            dma((3,)),
-            dma((2, Z)),
-            dma((2, Z)),
-            dma((2, R, Z)),
-            dma((2, R, Z)),
+            dma((4,)),
+            dma((2, Z - 1, 2, PIECES)),
+            dma((2, Z - 1, 2, PIECES)),
+            dma((2, R, Z, PIECES)),
+            dma((2, R, Z, PIECES)),
+            dma((T, PIECES)),
+            dma((T, PIECES)),
             dma((T,)),
             dma((T,)),
-            dma((T,)),
-            dma((T,)),
-            dma((4,)),
-            dma((4,)),
-            dma((Z,)),
-            dma((Z,)),
-            dma((R, Z)),
-            dma((R, Z)),
+            dma((4 + STRIPS,)),
+            dma((4 + STRIPS,)),
+            dma((STRIPS, Z)),
+            dma((STRIPS, Z)),
+            dma((STRIPS, R, Z)),
+            dma((STRIPS, R, Z)),
         ],
         compiler_params=pltpu.CompilerParams(
             collective_id=0, has_side_effects=True, vmem_limit_bytes=67043328
@@ -484,10 +571,9 @@
     )(
         attn_out,
         hidden_in,
-        routes,
         routes.T,
         norm_gain.reshape(1, D),
-        router,
+        router_weight.T,
         out_weight,
         gate_weight,
         up_weight,

time: 90.8 us -> 72.2 us (0.80)
  Pallas kernels: 76.1 us -> 62.7 us
  other arithmetic: 5.65 us -> 1.96 us
  local copies, waits for them, and re-layouts: 4.71 us -> 2.39 us
    pallas_call x1, Pallas kernels: 76.1 us -> 62.7 us  [local(): pl.pallas_call(functools.partial(body, (T, Z, R, rows, cap)), out_shape=j...]
    concatenate x1 -> x0, other arithmetic: 3.04 us -> none  [local(): jnp.concatenate([first, second, third, jnp.zeros((D, 128 - 3 * Z), f32)],...]
    another operation x2 -> x0, other arithmetic: 1.48 us -> none
    unnamed x15 -> x3, local copies, waits for them, and re-layouts: 2.95 us -> 1.62 us
where the time goes in v2:
time: 72.2 us; the launch traced here: 71.9 us
  Pallas kernels  62.7 us (87%)
  matrix products  4.77 us (7%)
  local copies, waits for them, and re-layouts  2.39 us (3%)
  other arithmetic  1.96 us (3%)
    pallas_call x1, Pallas kernels, local(): pl.pallas_call(functools.partial(body, (T, Z, R, rows, cap)), out_shape=j...  62.7 us
    dot_general x1, matrix products, attend(): jnp.einsum('skgd,skpd->skgp', grouped, cache_keys, preferred_element_type...  2.95 us
    unnamed x3, local copies, waits for them, and re-layouts  1.62 us

profile of v2, /device:TPU:0, one launch (start us, length us, event | category | flops | bytes accessed | tf_op | source)
XLA Modules:
  0.0 71.9 jit_solution(683589956598218466)
XLA Ops:
  0.0 0.0 copy-start
  0.0 0.9 %iota_compare_fusion = pred[32,128]{1,0:T(8,128)(4,1)S(1)} fusion(s32[32]{0:T(128)} %param.20), kind=kLoop, calls=%fused_computation.16 | loop fusion | flops 4096 | bytes 4224 | tf_op jit(solution)/shard_map/lt | solution.py:27
  0.9 1.1 %fusion.3 = f32[32,2,1,6]{3,2,1,0:T(1,128)S(1)} fusion(bf16[32,2,6,128]{3,0,2,1:T(8,128)(2,1)} %bitcast.9, bf16[32,2,128,1]{2,1,0,3:T(2,128)(2,1)} %bitcast.16), kind=kOutput, calls=%fused_computation.7 | convolution fusion | flops 98304 | bytes 116224 | tf_op jit(solution)/shard_map/skgd,skd->skg/dot_general | solution.py:30
  2.0 0.7 %convert_element_type.18 = f32[32,2,128]{2,1,0:T(2,128)S(1)} convert(bf16[32,2,128]{2,1,0:T(2,128)(2,1)} %param.17) | non-fusion elementwise | flops 8192 | bytes 49152 | tf_op jit(solution)/shard_map/convert_element_type | solution.py:43
  2.7 2.9 %fusion.11 = (f32[32,2,6]{2,1,0:T(2,128)S(1)}, f32[32,2,6,128]{3,2,1,0:T(8,128)S(1)}) fusion(bf16[32,2,128,128]{3,2,1,0:T(8,128)(2,1)} %param.18, bf16[32,2,6,128]{3,0,2,1:T(8,128)(2,1)} %bitcast.10, pred[32,128]{1,0:T(8,128)(4,1)S(1)} %iota_compare_fusion), kind=kOutput, calls=%fused_computation.19 | convolution fusion | flops 12729984 | bytes 2397696 | tf_op jit(solution)/shard_map/skgd,skpd->skgp/dot_general | solution.py:24
  5.7 0.3 fusion.2
  6.0 0.1 fusion.10
  6.0 0.0 copy-done
  6.1 0.7 %fusion.1 = bf16[32,2,6,128]{3,2,1,0:T(8,128)(2,1)S(1)} fusion(bf16[32,2,128,128]{3,2,1,0:T(8,128)(2,1)S(1)} %copy-done, f32[32,2,6,128]{3,2,1,0:T(8,128)S(1)} %get-tuple-element.8, f32[32,2,128]{2,1,0:T(2,128)S(1)} %convert_element_type.18, f32[32,2,6]{2,1,0:T(2,128)S(1)} %get-tuple-element.6, f32[32,2,6]{2,1,0:T(2,128)S(1)} %get-tuple-element.5, ...), kind=kOutput, calls=%fused_computation.3 | convolution fusion | flops 12877824 | bytes 2429440 | tf_op jit(solution)/shard_map/skgp,skpd->skgd/dot_general | solution.py:38
  6.8 0.8 %reshape.31.attn_ref = bf16[32,1536]{1,0:T(8,128)(2,1)} reshape(bf16[32,2,6,128]{3,2,1,0:T(8,128)(2,1)S(1)} %fusion.1) | data formatting | bytes 196608 | tf_op jit(solution)/shard_map/reshape | solution.py:45
  7.6 62.7 %shard_map.136 = bf16[32,3072]{1,0:T(8,128)(2,1)} custom-call(bf16[32,1536]{1,0:T(8,128)(2,1)} %reshape.31.attn_ref, bf16[32,3072]{1,0:T(8,128)(2,1)} %hidden_ref.1, s32[2,256]{1,0:T(2,128)} %bitcast.15, f32[1,3072]{1,0:T(1,128)} %bitcast.14, f32[4,3072]{1,0:T(4,128)} %bitcast.13, bf16[1536,384]{1,0:T(8,128)(2,1)} %out_hbm.1, bf16[3072,2048]{1,0:T(8,128)(2,1)} %gate_hbm.1, ...), custom_call_target="tpu_custom_call" | custom-call | tf_op jit(solution)/shard_map/pallas_call | solution.py:525
  70.3 1.6 %copy.28 = bf16[32,3072]{1,0:T(8,128)(2,1)} copy(bf16[32,3072]{1,0:T(8,128)(2,1)} %shard_map.136) | data formatting | bytes 393216
  (1 shorter events, 0.0 us)
Async XLA Ops:
  0.0 6.0 %copy-start = (bf16[32,2,128,128]{3,2,1,0:T(8,128)(2,1)S(1)}, bf16[32,2,128,128]{3,2,1,0:T(8,128)(2,1)}, u32[]{:S(2)}) copy-start(bf16[32,2,128,128]{3,2,1,0:T(8,128)(2,1)} %param.19) | copy-start | bytes 6291460
